TPU v7x, 32 devices: a whole 2x2x4 slice. The times are simulated.
32 devices in a mesh: wide: 16 (over z, y, x), narrow: 2 (over core).
Axes of the slice: x: 2, y: 2, z: 4, core: 2. Of those that a mesh axis runs over, the one named last changes fastest.
Arguments:
- features: bfloat16 [512, 16384], P('wide', 'narrow'), may hold values from -6 to 6
- queries: bfloat16 [1024, 16384], P('wide', 'narrow'), may hold values from -6 to 6
- damping: float32 [16384], P('wide'), may hold values from 0.25 to 4
Outputs:
- kernel: float32 [16384, 16384], P('wide', 'narrow')
- factor: float32 [16384, 256], P('wide')
- scores: float32 [1024, 512], P('wide', 'narrow')
All inputs are finite; a program needn't handle non-finite values.
Results may differ from a plain program's by a relative error of at most 0.0003.
Values may be sent and summed in bfloat16 or wider, within the bound.
No kernel may reach another device: no remote copies, remote signals or barrier semaphores. Data moves between devices by JAX's collectives and lax.ppermute only.
A program may use at most 128 MiB of HBM per device.

v0:
```python
import math
import jax
import jax.numpy as jnp
from jax import lax
from jax.sharding import PartitionSpec as P

P_SIZE = 16384
PANEL = 128
PANELS = 2


def broadcast(x, axis, root):
    mine = lax.axis_index(axis) == root
    return lax.psum(jnp.where(mine, x, jnp.zeros_like(x)), axis)


def on_device(features, queries, damping):
    rows_here = damping.shape[0]
    cols_here = queries.shape[1]
    slab_total = features.shape[0] * lax.axis_size("wide")
    wide_pos = lax.axis_index("wide")
    narrow_pos = lax.axis_index("narrow")
    contract_rows = (((0,), (0,)), ((), ()))
    contract_cols = (((1,), (1,)), ((), ()))
    full_width = lax.all_gather(features, "narrow", axis=1, tiled=True)
    row_features = lax.all_to_all(full_width, "wide", split_axis=1, concat_axis=0, tiled=True)
    slab_columns = lax.all_gather(features, "wide", axis=0, tiled=True)
    products = lax.dot_general(
        row_features, slab_columns, contract_rows, preferred_element_type=jnp.float32
    )
    partial_value = lax.dot_general(
        queries, slab_columns, contract_cols, preferred_element_type=jnp.float32
    )
    scores = lax.psum_scatter(partial_value, "narrow", scatter_dimension=1, tiled=True) * (
        1.0 / math.sqrt(P_SIZE)
    )
    row_ids = wide_pos * rows_here + lax.broadcasted_iota(jnp.int32, (rows_here, 1), 0)
    col_ids = narrow_pos * cols_here + lax.broadcasted_iota(jnp.int32, (1, cols_here), 1)
    kernel_block = products / slab_total + jnp.where(
        row_ids == col_ids, damping[:, None], jnp.float32(0.0)
    )
    factors = []
    for panel_index in range(PANELS):
        offset = panel_index * PANEL
        column_root = offset // cols_here
        row_root = offset // rows_here
        col_shift = offset % cols_here
        row_shift = offset % rows_here
        panel_columns = broadcast(
            kernel_block[:, col_shift : col_shift + PANEL], "narrow", column_root
        )
        pivot_block = broadcast(panel_columns[row_shift : row_shift + PANEL], "wide", row_root)
        pivot_factor = jnp.linalg.cholesky(pivot_block)
        lower_rows = lax.linalg.triangular_solve(
            pivot_factor, panel_columns, left_side=False, lower=True, transpose_a=True
        )
        pivot_rows = broadcast(kernel_block[row_shift : row_shift + PANEL], "wide", row_root)
        lower_cols = lax.linalg.triangular_solve(
            pivot_factor, pivot_rows, left_side=True, lower=True, transpose_a=False
        ).T
        kernel_block = kernel_block - jnp.dot(
            lower_rows,
            lower_cols.T,
            precision=lax.Precision.HIGHEST,
            preferred_element_type=jnp.float32,
        )
        boundary = offset + PANEL
        kernel_block = jnp.where(
            (row_ids < boundary) | (col_ids < boundary), jnp.zeros_like(kernel_block), kernel_block
        )
        factors.append(lower_rows)
    return (kernel_block, jnp.concatenate(factors, axis=1), scores)


def solution(mesh):
    return jax.shard_map(
        on_device,
        mesh=mesh,
        in_specs=(P("wide", "narrow"), P("wide", "narrow"), P("wide")),
        out_specs=(P("wide", "narrow"), P("wide", None), P("wide", "narrow")),
        check_vma=False,
    )
```

profile of v0, /device:TPU:0, one launch (start us, length us, event | category | flops | bytes accessed | tf_op | source)
XLA Modules:
  0.0 752.9 jit_solution(7625984602944274443)
XLA Ops:
  8.7 12.7 %all-gather.3.cloned.1.call-done = bf16[32,16384]{1,0:T(8,128)(2,1)} async-done(((bf16[32,8192]{1,0:T(8,128)(2,1)}), bf16[32,16384]{1,0:T(8,128)(2,1)}) %all-gather.3.cloned.1.call-update) | async-done | bytes 1048592 | tf_op jit(solution)/shard_map/all_gather | solution.py:25
  21.3 2.3 copy.41
  23.6 6.8 all-to-all-start
  30.5 35.8 %all-to-all-done = bf16[32,16,1024]{2,0,1:T(8,128)(2,1)S(1)} async-done(((bf16[32,16,1024]{2,0,1:T(8,128)(2,1)}), bf16[32,16,1024]{2,0,1:T(8,128)(2,1)S(1)}, u32[]{:S(2)}, u32[]{:S(2)}) %all-to-all-start) | async-done | bytes 1048608 | tf_op jit(solution)/shard_map/all_to_all | solution.py:26
  66.3 85.7 %all-gather.5.cloned.1.call-done = bf16[512,8192]{1,0:T(8,128)(2,1)} async-done(((bf16[32,8192]{1,0:T(8,128)(2,1)}), bf16[512,8192]{1,0:T(8,128)(2,1)}) %all-gather.5.cloned.1.call-update) | async-done | bytes 8388624 | tf_op jit(solution)/shard_map/all_gather | solution.py:27
  151.9 19.3 %select_add_fusion = f32[1024,8192]{0,1:T(8,128)} fusion(bf16[512,1024]{1,0:T(8,128)(2,1)S(1)} %bitcast.49, bf16[512,8192]{1,0:T(8,128)(2,1)} %all-gather.5.cloned.1.call-done, f32[1024]{0:T(1024)} %param.10, s32[1024]{0:T(1024)S(1)} %iota_add_fusion.1, s32[8192]{0:T(1024)S(1)} %iota_add_fusion), kind=kOutput, calls=%fused_computation.2 | convolution fusion | flops 8623489024 | bytes 43032576 | tf_op jit(solution)/shard_map/dot_general | solution.py:28
  171.3 1.9 slice_select_fusion.3
  173.2 4.4 slice_select_fusion.1
  177.6 12.5 %all-reduce.7.cloned.1.call-done = f32[1024,128]{0,1:T(8,128)} async-done(((f32[1024,128]{0,1:T(8,128)}), f32[1024,128]{0,1:T(8,128)}) %all-reduce.7.cloned.1.call-update) | async-done | bytes 524304 | tf_op jit(solution)/shard_map/psum | solution.py:14
  190.1 1.5 slice_select_fusion.5
  192.1 175.9 %all-reduce.13.cloned.1.call-done = (f32[128,128]{0,1:T(8,128)}, f32[128,8192]{0,1:T(8,128)}) async-done(((f32[128,128]{0,1:T(8,128)}, f32[128,8192]{0,1:T(8,128)}), (f32[128,128]{0,1:T(8,128)}, f32[128,8192]{0,1:T(8,128)})) %all-reduce.13.cloned.1.call-update) | async-done | bytes 4259856 | tf_op jit(solution)/shard_map/psum | solution.py:14
  368.0 0.9 copy.30
  368.9 0.9 fusion.9
  369.7 11.7 %cholesky.44 = f32[128,128]{1,0:T(8,128)S(1)} custom-call(f32[128,128]{1,0:T(8,128)S(1)} %fusion.9), custom_call_target="Cholesky" | custom-call | tf_op jit(solution)/shard_map/jit(cholesky)/cholesky | solution.py:53
  382.8 9.8 %custom-call.10 = f32[1,128,128]{1,2,0:T(8,128)S(1)} custom-call(f32[1,128,128]{2,1,0:T(8,128)S(1)} %fusion), custom_call_target="InvertDiagBlocksLowerTriangular" | custom-call | tf_op jit(solution)/shard_map/triangular_solve/custom-call.0 | solution.py:54
  392.6 6.1 fusion.6
  399.3 35.1 %subtract_select_fusion.1 = f32[1024,8192]{0,1:T(8,128)} fusion(f32[1024,8192]{0,1:T(8,128)} %select_add_fusion, f32[1024,128]{0,1:T(8,128)S(1)} %convolution_bitcast_fusion.1, f32[128,8192]{1,0:T(8,128)S(1)} %fusion.6, pred[1024]{0:T(1024)(128)(4,1)S(1)} %fusion.12, pred[8192]{0:T(1024)(128)(4,1)S(1)} %fusion.10), kind=kOutput, calls=%fused_computation.1 | convolution fusion | flops 12910067712 | bytes 71836672 | tf_op jit(solution)/shard_map/dot_general | solution.py:61
  434.5 1.9 slice_select_fusion.2
  436.4 6.7 fusion.14
  443.4 4.4 slice_select_fusion
  447.8 6.4 all-reduce.9.cloned.1.call-done
  454.2 1.5 slice_select_fusion.4
  455.8 9.3 %reduce-scatter.2.cloned.1.call-done = f32[64,256]{1,0:T(8,128)} async-done(((f32[64,512]{1,0:T(8,128)}), f32[64,256]{1,0:T(8,128)}) %reduce-scatter.2.cloned.1.call-update) | async-done | bytes 65552 | tf_op jit(solution)/shard_map/reduce_scatter | solution.py:34
  465.1 1.5 broadcast_multiply_fusion
  466.5 176.4 %all-reduce.11.cloned.1.call-done = (f32[128,128]{0,1:T(8,128)}, f32[128,8192]{0,1:T(8,128)}) async-done(((f32[128,128]{0,1:T(8,128)}, f32[128,8192]{0,1:T(8,128)}), (f32[128,128]{0,1:T(8,128)}, f32[128,8192]{0,1:T(8,128)})) %all-reduce.11.cloned.1.call-update) | async-done | bytes 4259856 | tf_op jit(solution)/shard_map/psum | solution.py:14
  643.0 0.9 copy.32
  644.7 11.7 %cholesky.55 = f32[128,128]{1,0:T(8,128)S(1)} custom-call(f32[128,128]{1,0:T(8,128)S(1)} %fusion.5), custom_call_target="Cholesky" | custom-call | tf_op jit(solution)/shard_map/jit(cholesky)/cholesky | solution.py:53
  657.8 9.8 %custom-call.12 = f32[1,128,128]{1,2,0:T(8,128)S(1)} custom-call(f32[1,128,128]{2,1,0:T(8,128)S(1)} %fusion.1), custom_call_target="InvertDiagBlocksLowerTriangular" | custom-call | tf_op jit(solution)/shard_map/triangular_solve/custom-call.0 | solution.py:54
  667.6 8.0 %fusion.2 = f32[128,8192]{1,0:T(8,128)} fusion(f32[128,8192]{0,1:T(8,128)} %get-tuple-element.19, f32[1,128,128]{1,2,0:T(8,128)S(1)} %custom-call.12), kind=kOutput, calls=%fused_computation.17 | convolution fusion | flops 1610612736 | bytes 8454144 | tf_op jit(solution)/shard_map/triangular_solve/dot.0 | solution.py:58
  676.3 1.3 copy.35
  677.7 37.0 %subtract_select_fusion = f32[1024,8192]{0,1:T(8,128)} fusion(f32[1024,8192]{0,1:T(8,128)} %subtract_select_fusion.1, f32[1024,128]{0,1:T(8,128)S(1)} %convolution_bitcast_fusion, f32[128,8192]{1,0:T(8,128)} %fusion.2, pred[1024]{0:T(1024)(128)(4,1)S(1)} %fusion.13, pred[8192]{0:T(1024)(128)(4,1)S(1)} %fusion.11), kind=kOutput, calls=%fused_computation | convolution fusion | flops 12910067712 | bytes 71836672 | tf_op jit(solution)/shard_map/dot_general | solution.py:61
  714.6 31.2 %copy.34 = f32[1024,8192]{1,0:T(8,128)} copy(f32[1024,8192]{0,1:T(8,128)} %subtract_select_fusion) | data formatting | bytes 67108864
  (38 shorter events, 7.1 us)
Async XLA Ops:
  7.2 429.3 %copy-start = (bf16[64,8192]{1,0:T(8,128)(2,1)S(1)}, bf16[64,8192]{1,0:T(8,128)(2,1)}, u32[]{:S(2)}) copy-start(bf16[64,8192]{1,0:T(8,128)(2,1)} %param.9) | copy-start | bytes 3145732
  7.2 14.1 %all-gather.3.cloned.1.call-start = ((), (), s32[]{:S(2)}) async-start(), calls=%async_computation.2 | async-start | bytes 1572864 | tf_op jit(solution)/shard_map/all_gather | solution.py:25
  7.9 144.0 %all-gather.5.cloned.1.call-start = ((), (), s32[]{:S(2)}) async-start(), calls=%async_computation.3 | async-start | bytes 8912896 | tf_op jit(solution)/shard_map/all_gather | solution.py:27
  23.6 42.7 %all-to-all-start = ((bf16[32,16,1024]{2,0,1:T(8,128)(2,1)}), bf16[32,16,1024]{2,0,1:T(8,128)(2,1)S(1)}, u32[]{:S(2)}, u32[]{:S(2)}) async-start(bf16[32,16,1024]{2,0,1:T(8,128)(2,1)} %bitcast.48), calls=%async_computation | async-start | bytes 2097152 | tf_op jit(solution)/shard_map/all_to_all | solution.py:26
  30.4 159.7 %all-reduce.7.cloned.1.call-start = ((), (), s32[]{:S(2)}) async-start(), calls=%async_computation.4 | async-start | bytes 1048576 | tf_op jit(solution)/shard_map/psum | solution.py:14
  173.2 194.8 %all-reduce.13.cloned.1.call-start = ((), (), s32[]{:S(2)}) async-start(), calls=%async_computation.8 | async-start | bytes 8519680 | tf_op jit(solution)/shard_map/psum | solution.py:14
  190.1 208.6 %copy-start.3 = (f32[1024,128]{0,1:T(8,128)S(1)}, f32[1024,128]{0,1:T(8,128)}, u32[]{:S(2)}) copy-start(f32[1024,128]{0,1:T(8,128)} %all-reduce.7.cloned.1.call-done) | copy-start | bytes 1572868
  191.7 262.5 %all-reduce.9.cloned.1.call-start = ((), (), s32[]{:S(2)}) async-start(), calls=%async_computation.5 | async-start | bytes 1048576 | tf_op jit(solution)/shard_map/psum | solution.py:14
  436.4 28.7 %reduce-scatter.2.cloned.1.call-start = ((), (), s32[]{:S(2)}) async-start(), calls=%async_computation.6 | async-start | bytes 196608 | tf_op jit(solution)/shard_map/reduce_scatter | solution.py:34
  443.2 199.8 %all-reduce.11.cloned.1.call-start = ((), (), s32[]{:S(2)}) async-start(), calls=%async_computation.7 | async-start | bytes 8519680 | tf_op jit(solution)/shard_map/psum | solution.py:14
  454.2 221.4 %copy-start.2 = (f32[1024,128]{0,1:T(8,128)S(1)}, f32[1024,128]{0,1:T(8,128)}, u32[]{:S(2)}) copy-start(f32[1024,128]{0,1:T(8,128)} %all-reduce.9.cloned.1.call-done) | copy-start | bytes 1572868
  714.6 31.2 %copy-start.1 = (bf16[64,8192]{1,0:T(8,128)(2,1)S(1)}, bf16[64,8192]{1,0:T(8,128)(2,1)}, u32[]{:S(2)}) copy-start(bf16[64,8192]{1,0:T(8,128)(2,1)} %param.9) | copy-start | bytes 3145732
Sparse Core Ops, SparseCore 0:
  9.5 11.7 all-gather.2
  24.1 127.8 all-gather.4
  173.3 16.7 all-reduce.6
  196.5 171.4 all-reduce.12
  436.5 17.6 all-reduce.8
  456.2 8.7 reduce-scatter.1
  471.6 171.3 all-reduce.10
where the time goes:
time: 759 us; the launch traced here: 753 us
  waiting for transfers between devices  516 us (68%)
  matrix products  113 us (15%)
  other arithmetic  64.7 us (9%)
  local copies, waits for them, and re-layouts  36.6 us (5%)
  between operations  14.5 us (2%)
    psum x4, waiting for transfers between devices, broadcast(): return lax.psum(jnp.where(mine, x, jnp.zeros_like(x)), axis)  371 us
    all_gather x1, waiting for transfers between devices, on_device(): slab_columns = lax.all_gather(features, 'wide', axis=0, tiled=True)  85.7 us
    dot_general x2, matrix products, on_device(): jnp.dot(lower_rows, lower_cols.T, precision=lax.Precision.HIGHEST, prefer...  72.1 us
    all_to_all x1, waiting for transfers between devices, on_device(): lax.all_to_all(full_width, 'wide', split_axis=1, concat_axis=0, tiled=True)  35.8 us
    unnamed x10, local copies, waits for them, and re-layouts  32.5 us
    another operation x6, other arithmetic, on_device(): pivot_factor = jnp.linalg.cholesky(pivot_block)  24.8 us
    another operation x4, other arithmetic, on_device(): lax.linalg.triangular_solve(pivot_factor, panel_columns, left_side=False,...  20.9 us
    dot_general x1, matrix products, on_device(): lax.dot_general(row_features, slab_columns, contract_rows, preferred_elem...  19.3 us
  transfers between devices with their start and end apart: 8, of which 8 were waited for; matrix products, arithmetic and copies ran while one was open for 3% of the time, Pallas kernels for 0%

commit v1 on v0

--- a/solution.py
+++ b/solution.py
@@ -24,7 +24,9 @@
     contract_cols = (((1,), (1,)), ((), ()))
     full_width = lax.all_gather(features, "narrow", axis=1, tiled=True)
     row_features = lax.all_to_all(full_width, "wide", split_axis=1, concat_axis=0, tiled=True)
-    slab_columns = lax.all_gather(features, "wide", axis=0, tiled=True)
+    slab_columns = jnp.concatenate(
+        lax.all_to_all(jnp.stack([features] * lax.axis_size("wide")), "wide", 0, 0), axis=0
+    )
     products = lax.dot_general(
         row_features, slab_columns, contract_rows, preferred_element_type=jnp.float32
     )

time: 759 us -> 863 us (1.14)
  waiting for transfers between devices: 516 us -> 583 us
  blocking collectives: 0 us -> 33.3 us
    all_to_all x1, waiting for transfers between devices: 35.8 us -> 153 us  [on_device(): lax.all_to_all(jnp.stack([features] * lax.axis_size('wide')), 'wide', 0, 0)]
    all_gather x1 -> x0, waiting for transfers between devices: 85.7 us -> none  [on_device(): slab_columns = lax.all_gather(features, 'wide', axis=0, tiled=True)]
    psum x4, waiting for transfers between devices: 371 us -> 407 us  [broadcast(): return lax.psum(jnp.where(mine, x, jnp.zeros_like(x)), axis)]
    all_to_all x0 -> x1, blocking collectives: none -> 33.3 us  [on_device(): lax.all_to_all(full_width, 'wide', split_axis=1, concat_axis=0, tiled=True)]
    unnamed x10 -> x12, local copies, waits for them, and re-layouts: 32.5 us -> 32.5 us
  transfers between devices with their start and end apart: 8 -> 7, of which waited for: 8 -> 7; matrix products, arithmetic and copies ran while one was open for 3% -> 2% of each run, Pallas kernels for 0% -> 0%
where the time goes in v1:
time: 863 us; the launch traced here: 856 us
  waiting for transfers between devices  583 us (68%)
  matrix products  114 us (13%)
  other arithmetic  64.7 us (7%)
  local copies, waits for them, and re-layouts  41.1 us (5%)
  blocking collectives  33.3 us (4%)
  between operations  14.5 us (2%)
    psum x4, waiting for transfers between devices, broadcast(): return lax.psum(jnp.where(mine, x, jnp.zeros_like(x)), axis)  407 us
    all_to_all x1, waiting for transfers between devices, on_device(): lax.all_to_all(jnp.stack([features] * lax.axis_size('wide')), 'wide', 0, 0)  153 us
    dot_general x2, matrix products, on_device(): jnp.dot(lower_rows, lower_cols.T, precision=lax.Precision.HIGHEST, prefer...  72.1 us
    all_to_all x1, blocking collectives, on_device(): lax.all_to_all(full_width, 'wide', split_axis=1, concat_axis=0, tiled=True)  33.3 us
    unnamed x12, local copies, waits for them, and re-layouts  32.5 us
    another operation x6, other arithmetic, on_device(): pivot_factor = jnp.linalg.cholesky(pivot_block)  24.8 us
    another operation x4, other arithmetic, on_device(): lax.linalg.triangular_solve(pivot_factor, panel_columns, left_side=False,...  20.9 us
    dot_general x1, matrix products, on_device(): lax.dot_general(row_features, slab_columns, contract_rows, preferred_elem...  19.4 us
  transfers between devices with their start and end apart: 7, of which 7 were waited for; matrix products, arithmetic and copies ran while one was open for 2% of the time, Pallas kernels for 0%

profile of v1, /device:TPU:0, one launch (start us, length us, event | category | flops | bytes accessed | tf_op | source)
XLA Modules:
  0.0 856.1 jit_solution(12248012027570586367)
XLA Ops:
  7.9 13.4 %all-gather.2.cloned.1.call-done = bf16[32,16384]{1,0:T(8,128)(2,1)} async-done(((bf16[32,8192]{1,0:T(8,128)(2,1)}), bf16[32,16384]{1,0:T(8,128)(2,1)}) %all-gather.2.cloned.1.call-update) | async-done | bytes 1048592 | tf_op jit(solution)/shard_map/all_gather | solution.py:25
  21.3 1.3 copy.27
  22.6 33.3 %all_to_all.21 = bf16[32,16,1024]{2,0,1:T(8,128)(2,1)S(1)} all-to-all(bf16[32,16,1024]{2,0,1:T(8,128)(2,1)S(1)} %bitcast.53), channel_id=1, replica_groups=mesh['wide'=16,'narrow'=2] {'wide'}, dimensions={1} | all-to-all | bytes 2097152 | tf_op jit(solution)/shard_map/all_to_all | solution.py:26
  55.9 5.5 stack.2
  61.4 4.9 all-to-all-start.1
  66.4 153.3 %all-to-all-done.1 = bf16[16,32,8192]{2,1,0:T(8,128)(2,1)} async-done(((bf16[16,32,8192]{2,1,0:T(8,128)(2,1)}), bf16[16,32,8192]{2,1,0:T(8,128)(2,1)}, u32[]{:S(2)}, u32[]{:S(2)}) %all-to-all-start.1) | async-done | bytes 8388640 | tf_op jit(solution)/shard_map/all_to_all | solution.py:28
  219.7 19.4 %fusion = f32[1024,8192]{0,1:T(8,128)} fusion(bf16[16,32,8192]{2,1,0:T(8,128)(2,1)} %all-to-all-done.1, f32[1024]{0:T(1024)S(1)} %copy-done.4, s32[1024]{0:T(1024)S(1)} %iota_add_fusion.1, s32[8192]{0:T(1024)S(1)} %iota_add_fusion, bf16[32,16,1024]{2,0,1:T(8,128)(2,1)S(1)} %all_to_all.21), kind=kOutput, calls=%fused_computation.1 | convolution fusion | flops 8623489024 | bytes 43032576 | tf_op jit(solution)/shard_map/dot_general | solution.py:30
  239.1 1.9 slice_select_fusion.3
  241.0 4.4 slice_select_fusion.1
  245.4 47.9 %all-reduce.7.cloned.1.call-done = f32[1024,128]{0,1:T(8,128)} async-done(((f32[1024,128]{0,1:T(8,128)}), f32[1024,128]{0,1:T(8,128)}) %all-reduce.7.cloned.1.call-update) | async-done | bytes 524304 | tf_op jit(solution)/shard_map/psum | solution.py:14
  293.4 1.5 slice_select_fusion.5
  295.3 176.0 %all-reduce.13.cloned.1.call-done = (f32[128,128]{0,1:T(8,128)}, f32[128,8192]{0,1:T(8,128)}) async-done(((f32[128,128]{0,1:T(8,128)}, f32[128,8192]{0,1:T(8,128)}), (f32[128,128]{0,1:T(8,128)}, f32[128,8192]{0,1:T(8,128)})) %all-reduce.13.cloned.1.call-update) | async-done | bytes 4259856 | tf_op jit(solution)/shard_map/psum | solution.py:14
  471.3 0.9 copy.15
  473.1 11.7 %cholesky.44 = f32[128,128]{1,0:T(8,128)S(1)} custom-call(f32[128,128]{1,0:T(8,128)S(1)} %fusion.11), custom_call_target="Cholesky" | custom-call | tf_op jit(solution)/shard_map/jit(cholesky)/cholesky | solution.py:55
  486.2 9.8 %custom-call.10 = f32[1,128,128]{1,2,0:T(8,128)S(1)} custom-call(f32[1,128,128]{2,1,0:T(8,128)S(1)} %fusion.2), custom_call_target="InvertDiagBlocksLowerTriangular" | custom-call | tf_op jit(solution)/shard_map/triangular_solve/custom-call.0 | solution.py:56
  496.0 6.1 fusion.8
  502.7 35.1 %subtract_select_fusion.1 = f32[1024,8192]{0,1:T(8,128)} fusion(f32[1024,8192]{0,1:T(8,128)} %fusion, f32[1024,128]{0,1:T(8,128)S(1)} %convolution_bitcast_fusion.1, f32[128,8192]{1,0:T(8,128)S(1)} %fusion.8, pred[1024]{0:T(1024)(128)(4,1)S(1)} %fusion.14, pred[8192]{0:T(1024)(128)(4,1)S(1)} %fusion.12), kind=kOutput, calls=%fused_computation.3 | convolution fusion | flops 12910067712 | bytes 71836672 | tf_op jit(solution)/shard_map/dot_general | solution.py:63
  537.9 1.9 slice_select_fusion.2
  539.8 6.7 fusion.16
  546.8 4.4 slice_select_fusion
  551.2 6.3 all-reduce.9.cloned.1.call-done
  557.6 1.5 slice_select_fusion.4
  559.2 9.3 %reduce-scatter.2.cloned.1.call-done = f32[64,256]{1,0:T(8,128)} async-done(((f32[64,512]{1,0:T(8,128)}), f32[64,256]{1,0:T(8,128)}) %reduce-scatter.2.cloned.1.call-update) | async-done | bytes 65552 | tf_op jit(solution)/shard_map/reduce_scatter | solution.py:36
  568.4 1.5 broadcast_multiply_fusion
  569.9 176.3 %all-reduce.11.cloned.1.call-done = (f32[128,128]{0,1:T(8,128)}, f32[128,8192]{0,1:T(8,128)}) async-done(((f32[128,128]{0,1:T(8,128)}, f32[128,8192]{0,1:T(8,128)}), (f32[128,128]{0,1:T(8,128)}, f32[128,8192]{0,1:T(8,128)})) %all-reduce.11.cloned.1.call-update) | async-done | bytes 4259856 | tf_op jit(solution)/shard_map/psum | solution.py:14
  746.2 0.9 copy.17
  748.0 11.7 %cholesky.55 = f32[128,128]{1,0:T(8,128)S(1)} custom-call(f32[128,128]{1,0:T(8,128)S(1)} %fusion.7), custom_call_target="Cholesky" | custom-call | tf_op jit(solution)/shard_map/jit(cholesky)/cholesky | solution.py:55
  761.0 9.8 %custom-call.12 = f32[1,128,128]{1,2,0:T(8,128)S(1)} custom-call(f32[1,128,128]{2,1,0:T(8,128)S(1)} %fusion.3), custom_call_target="InvertDiagBlocksLowerTriangular" | custom-call | tf_op jit(solution)/shard_map/triangular_solve/custom-call.0 | solution.py:56
  770.8 8.0 fusion.4
  779.6 1.3 copy.20
  780.9 37.0 %subtract_select_fusion = f32[1024,8192]{0,1:T(8,128)} fusion(f32[1024,8192]{0,1:T(8,128)} %subtract_select_fusion.1, f32[1024,128]{0,1:T(8,128)S(1)} %convolution_bitcast_fusion, f32[128,8192]{1,0:T(8,128)} %fusion.4, pred[1024]{0:T(1024)(128)(4,1)S(1)} %fusion.15, pred[8192]{0:T(1024)(128)(4,1)S(1)} %fusion.13), kind=kOutput, calls=%fused_computation.2 | convolution fusion | flops 12910067712 | bytes 71836672 | tf_op jit(solution)/shard_map/dot_general | solution.py:63
  817.8 31.2 %copy.19 = f32[1024,8192]{1,0:T(8,128)} copy(f32[1024,8192]{0,1:T(8,128)} %subtract_select_fusion) | data formatting | bytes 67108864
  (39 shorter events, 7.3 us)
Async XLA Ops:
  7.2 532.7 %copy-start = (bf16[64,8192]{1,0:T(8,128)(2,1)S(1)}, bf16[64,8192]{1,0:T(8,128)(2,1)}, u32[]{:S(2)}) copy-start(bf16[64,8192]{1,0:T(8,128)(2,1)} %param.9) | copy-start | bytes 3145732
  7.2 14.1 %all-gather.2.cloned.1.call-start = ((), (), s32[]{:S(2)}) async-start(), calls=%async_computation.3 | async-start | bytes 1572864 | tf_op jit(solution)/shard_map/all_gather | solution.py:25
  61.4 158.2 %copy-start.4 = (f32[1024]{0:T(1024)S(1)}, f32[1024]{0:T(1024)}, u32[]{:S(2)}) copy-start(f32[1024]{0:T(1024)} %param.10) | copy-start | bytes 12292
  61.4 158.2 %all-to-all-start.1 = ((bf16[16,32,8192]{2,1,0:T(8,128)(2,1)}), bf16[16,32,8192]{2,1,0:T(8,128)(2,1)}, u32[]{:S(2)}, u32[]{:S(2)}) async-start(bf16[16,32,8192]{2,1,0:T(8,128)(2,1)} %stack.2), calls=%async_computation.1 | async-start | bytes 16777216 | tf_op jit(solution)/shard_map/all_to_all | solution.py:28
  66.3 227.0 %all-reduce.7.cloned.1.call-start = ((), (), s32[]{:S(2)}) async-start(), calls=%async_computation.4 | async-start | bytes 1048576 | tf_op jit(solution)/shard_map/psum | solution.py:14
  241.0 230.4 %all-reduce.13.cloned.1.call-start = ((), (), s32[]{:S(2)}) async-start(), calls=%async_computation.8 | async-start | bytes 8519680 | tf_op jit(solution)/shard_map/psum | solution.py:14
  293.4 208.7 %copy-start.3 = (f32[1024,128]{0,1:T(8,128)S(1)}, f32[1024,128]{0,1:T(8,128)}, u32[]{:S(2)}) copy-start(f32[1024,128]{0,1:T(8,128)} %all-reduce.7.cloned.1.call-done) | copy-start | bytes 1572868
  294.9 262.6 %all-reduce.9.cloned.1.call-start = ((), (), s32[]{:S(2)}) async-start(), calls=%async_computation.5 | async-start | bytes 1048576 | tf_op jit(solution)/shard_map/psum | solution.py:14
  539.8 28.7 %reduce-scatter.2.cloned.1.call-start = ((), (), s32[]{:S(2)}) async-start(), calls=%async_computation.6 | async-start | bytes 196608 | tf_op jit(solution)/shard_map/reduce_scatter | solution.py:36
  546.5 199.6 %all-reduce.11.cloned.1.call-start = ((), (), s32[]{:S(2)}) async-start(), calls=%async_computation.7 | async-start | bytes 8519680 | tf_op jit(solution)/shard_map/psum | solution.py:14
  557.5 221.3 %copy-start.2 = (f32[1024,128]{0,1:T(8,128)S(1)}, f32[1024,128]{0,1:T(8,128)}, u32[]{:S(2)}) copy-start(f32[1024,128]{0,1:T(8,128)} %all-reduce.9.cloned.1.call-done) | copy-start | bytes 1572868
  817.8 31.2 %copy-start.1 = (bf16[64,8192]{1,0:T(8,128)(2,1)S(1)}, bf16[64,8192]{1,0:T(8,128)(2,1)}, u32[]{:S(2)}) copy-start(bf16[64,8192]{1,0:T(8,128)(2,1)} %param.9) | copy-start | bytes 3145732
Sparse Core Ops, SparseCore 0:
  9.5 11.7 all-gather.1
  241.1 52.2 all-reduce.6
  299.9 171.4 all-reduce.12
  539.9 17.6 all-reduce.8
  559.6 8.7 reduce-scatter.1
  574.8 171.3 all-reduce.10
